TPU v7x, 256 devices: a whole 4x4x8 slice. The times are simulated.
256 devices in a mesh: rows: 2 (over core), cols: 4 (over y), slabs: 8 (over z), site: 4 (over x).
Axes of the slice: x: 4, y: 4, z: 8, core: 2. Of those that a mesh axis runs over, the one named last changes fastest.
Arguments:
- field_values: float32 [768, 32, 64, 128], P(('site', 'rows'), 'cols', 'slabs'), parts along dimension 0, may hold values from 0.5 to 2
- crowding: float32 [768, 32, 64, 128], P(('site', 'rows'), 'cols', 'slabs'), parts along dimension 0, may hold values from 0.5 to 2
Outputs:
- standardized: float32 [768, 32, 64, 128], P(('site', 'rows'), 'cols', 'slabs'), parts along dimension 0
- field_values_end: float32 [768, 32, 64, 128], P(('site', 'rows'), 'cols', 'slabs'), parts along dimension 0
There are 4 independent parts, one for each index of `site`. A program takes and returns all parts, laid end to end along the dimension named above; each array names one. Nothing has to cross between parts.
All inputs are finite; a program needn't handle non-finite values.
Results may differ from a plain program's by a relative error of at most 0.000036.
Values sent between devices are 32-bit elements; how exact they have to be, the bound alone decides.
A program may use at most 64 MiB of HBM per device.

v0:
```python
import functools

import jax
import jax.numpy as jnp
from jax import lax
from jax.experimental import pallas as pl
from jax.experimental.pallas import tpu as pltpu
from jax.sharding import PartitionSpec as P

STEPS = 6
CHUNKS = 6
MESH = pl.DeviceIdType.MESH
Z = 8


def evolve(sizes, f_hbm, c_hbm, end_ref, mean_ref, scale_ref, field, crowd, shift, first, second,
           mine, theirs, load_sem, crowd_sem, send_sem, recv_sem, row_send, row_recv, stat_send, stat_recv):
    rows, cols, slabs = sizes
    height, width, depth, _ = f_hbm.shape
    part = height // CHUNKS
    me_row, me_col, me_slab = (lax.axis_index(axis) for axis in ("rows", "cols", "slabs"))
    partner = {"rows": 1 - me_row}
    peers = (
        {"cols": lax.rem(me_col + cols - 1, cols)},
        {"cols": lax.rem(me_col + 1, cols)},
        {"slabs": lax.rem(me_slab + slabs - 1, slabs)},
        {"slabs": lax.rem(me_slab + 1, slabs)},
    )
    inner_x, inner_z = pl.ds(1, width), pl.ds(Z, depth)

    def load(chunk):
        return pltpu.make_async_copy(
            f_hbm.at[pl.ds(chunk * part, part)],
            field.at[0, pl.ds(1 + chunk * part, part), inner_x, inner_z],
            load_sem.at[chunk],
        )

    def load_crowd(chunk):
        part_rows = pl.ds(chunk * part, part)
        return pltpu.make_async_copy(c_hbm.at[part_rows], crowd.at[part_rows], crowd_sem.at[chunk])

    def face(slot, chunk, side):
        part_rows = pl.ds(1 + chunk * part, part)
        source, target = (
            ((1, inner_z), (width + 1, inner_z)),
            ((width, inner_z), (0, inner_z)),
            ((inner_x, Z), (inner_x, Z + depth)),
            ((inner_x, Z + depth - 1), (inner_x, Z - 1)),
        )[side]
        return pltpu.make_async_remote_copy(
            src_ref=field.at[(slot, part_rows) + source],
            dst_ref=field.at[(slot, part_rows) + target],
            send_sem=send_sem.at[slot, chunk, side],
            recv_sem=recv_sem.at[slot, chunk, side],
            device_id=peers[side],
            device_id_type=MESH,
        )

    def edge_row(slot, side):
        source, target = ((1, height + 1), (height, 0))[side]
        return pltpu.make_async_remote_copy(
            src_ref=field.at[slot, source, inner_x, inner_z],
            dst_ref=field.at[slot, target, inner_x, inner_z],
            send_sem=row_send.at[slot, side],
            recv_sem=row_recv.at[slot, side],
            device_id=partner,
            device_id_type=MESH,
        )

    def on_edges(chunk, act):
        @pl.when(chunk == 0)
        def _():
            act(0)

        @pl.when(chunk == CHUNKS - 1)
        def _():
            act(1)

    def send(slot, chunk):
        for side in range(4):
            face(slot, chunk, side).start()
        on_edges(chunk, lambda side: edge_row(slot, side).start())

    def sent(slot, chunk):
        for side in range(4):
            face(slot, chunk, side).wait_send()
        on_edges(chunk, lambda side: edge_row(slot, side).wait_send())

    def arrived(slot, chunk):
        for side in range(4):
            face(slot, chunk, side).wait_recv()
        on_edges(chunk, lambda side: edge_row(slot, 1 - side).wait_recv())

    def advance(slot, chunk, store):
        def row(step, _):
            y = chunk * part + step
            centre = [field[slot, y + 1, x, inner_z] for x in range(width + 2)]
            for x in range(width):
                value = centre[x + 1]
                around = (
                    (field[slot, y, x + 1, inner_z] + field[slot, y + 2, x + 1, inner_z])
                    + (centre[x] + centre[x + 2])
                    + (field[slot, y + 1, x + 1, pl.ds(Z - 1, depth)] + field[slot, y + 1, x + 1, pl.ds(Z + 1, depth)])
                )
                store(y, x, 0.1 * around + value * (0.6 - (0.2 * value) * crowd[y, x]))
            return 0

        lax.fori_loop(0, part, row, 0)

    for chunk in range(CHUNKS):
        load(chunk).start()
    for chunk in range(CHUNKS):
        load_crowd(chunk).start()

    barrier = pltpu.get_barrier_semaphore()
    for peer in peers + (partner,):
        pl.semaphore_signal(barrier, inc=1, device_id=peer, device_id_type=MESH)
    pl.semaphore_wait(barrier, len(peers) + 1)

    def begin(chunk, _):
        load(chunk).wait()
        send(0, chunk)
        return 0

    lax.fori_loop(0, CHUNKS, begin, 0)

    def loaded(chunk, _):
        load_crowd(chunk).wait()
        return 0

    lax.fori_loop(0, CHUNKS, loaded, 0)

    def one_step(step, _):
        slot = lax.rem(step, 2)
        other = 1 - slot

        def one_chunk(place, _):
            chunk = lax.rem(place + step, CHUNKS)
            arrived(slot, chunk)

            @pl.when(step > 0)
            def _():
                sent(other, chunk)

            def store(y, x, value):
                field[other, y + 1, x + 1, inner_z] = value

            advance(slot, chunk, store)
            send(other, chunk)
            return 0

        lax.fori_loop(0, CHUNKS, one_chunk, 0)
        return 0

    lax.fori_loop(0, STEPS - 1, one_step, 0)

    step = STEPS - 1
    slot = step % 2

    def last_chunk(place, _):
        chunk = lax.rem(place + step, CHUNKS)
        arrived(slot, chunk)

        def store(y, x, value):
            end_ref[y, x] = value

        advance(slot, chunk, store)

        @pl.when(place == 0)
        def _():
            for x in range(width):
                shift[x] = end_ref[chunk * part, x]
                first[x] = jnp.zeros_like(first[x])
                second[x] = jnp.zeros_like(second[x])

        for x in range(width):
            middle = shift[x]
            one, two = first[x], second[x]
            for y in range(part):
                moved = end_ref[chunk * part + y, x] - middle
                one, two = one + moved, two + moved * moved
            first[x], second[x] = one, two
        return 0

    lax.fori_loop(0, CHUNKS, last_chunk, 0)

    for x in range(width):
        mine[0, x] = shift[x] + first[x] * (1.0 / height)
        mine[1, x] = second[x] - first[x] * first[x] * (1.0 / height)
    swap = pltpu.make_async_remote_copy(
        src_ref=mine,
        dst_ref=theirs,
        send_sem=stat_send,
        recv_sem=stat_recv,
        device_id=partner,
        device_id_type=MESH,
    )
    swap.start()

    def drain(chunk, _):
        sent(1 - slot, chunk)
        sent(slot, chunk)
        return 0

    lax.fori_loop(0, CHUNKS, drain, 0)
    swap.wait()
    for x in range(width):
        apart = mine[0, x] - theirs[0, x]
        total = mine[1, x] + theirs[1, x] + apart * apart * (0.5 * height)
        mean_ref[x] = 0.5 * (mine[0, x] + theirs[0, x])
        scale_ref[x] = lax.rsqrt(total * (0.5 / height) + 0.0001)


def finish(end_ref, mean_ref, scale_ref, standardized_hbm, end_hbm, standardized, out_sem, end_sem):
    height, width = end_ref.shape[:2]
    part = height // CHUNKS
    copy_end = pltpu.make_async_copy(end_ref, end_hbm, end_sem)

    def copy_out(chunk):
        part_rows = pl.ds(chunk * part, part)
        return pltpu.make_async_copy(standardized.at[part_rows], standardized_hbm.at[part_rows], out_sem.at[chunk])

    copy_end.start()
    for chunk in range(CHUNKS):

        def row(step, _):
            y = chunk * part + step
            for x in range(width):
                standardized[y, x] = (end_ref[y, x] - mean_ref[x]) * scale_ref[x]
            return 0

        lax.fori_loop(0, part, row, 0)
        copy_out(chunk).start()
    for chunk in range(CHUNKS):
        copy_out(chunk).wait()
    copy_end.wait()


def local(sizes, field_values, crowding):
    height, width, depth, lanes = field_values.shape
    whole = jax.ShapeDtypeStruct(field_values.shape, jnp.float32)
    line = jax.ShapeDtypeStruct((width, depth, lanes), jnp.float32)
    vmem, anywhere = pl.BlockSpec(memory_space=pltpu.VMEM), pl.BlockSpec(memory_space=pl.ANY)
    plane = pltpu.VMEM((width, depth, lanes), jnp.float32)
    end, mean, scale = pl.pallas_call(
        functools.partial(evolve, sizes),
        out_shape=(whole, line, line),
        in_specs=[anywhere, anywhere],
        out_specs=(vmem, vmem, vmem),
        scratch_shapes=[
            pltpu.VMEM((2, height + 2, width + 2, 3 * depth, lanes), jnp.float32),
            pltpu.VMEM((height, width, depth, lanes), jnp.float32),
            plane,
            plane,
            plane,
            pltpu.VMEM((2, width, depth, lanes), jnp.float32),
            pltpu.VMEM((2, width, depth, lanes), jnp.float32),
            pltpu.SemaphoreType.DMA((CHUNKS,)),
            pltpu.SemaphoreType.DMA((CHUNKS,)),
            pltpu.SemaphoreType.DMA((2, CHUNKS, 4)),
            pltpu.SemaphoreType.DMA((2, CHUNKS, 4)),
            pltpu.SemaphoreType.DMA((2, 2)),
            pltpu.SemaphoreType.DMA((2, 2)),
            pltpu.SemaphoreType.DMA,
            pltpu.SemaphoreType.DMA,
        ],
        compiler_params=pltpu.CompilerParams(collective_id=0, has_side_effects=True),
        name="evolve",
    )(field_values, crowding)
    return pl.pallas_call(
        finish,
        out_shape=(whole, whole),
        in_specs=[vmem, vmem, vmem],
        out_specs=(anywhere, anywhere),
        scratch_shapes=[
            pltpu.VMEM((height, width, depth, lanes), jnp.float32),
            pltpu.SemaphoreType.DMA((CHUNKS,)),
            pltpu.SemaphoreType.DMA,
        ],
        name="finish",
    )(end, mean, scale)


def solution(mesh):
    spec = P(("site", "rows"), "cols", "slabs", None)
    sizes = tuple(mesh.shape[axis] for axis in ("rows", "cols", "slabs"))
    return jax.shard_map(
        functools.partial(local, sizes),
        mesh=mesh,
        in_specs=(spec, spec),
        out_specs=(spec, spec),
        check_vma=False,
    )
```

profile of v0, /device:TPU:1, one launch (start us, length us, event | category | flops | bytes accessed | tf_op | source)
XLA Modules:
  0.0 71.1 jit_solution(4992978992970886218)
XLA Ops:
  0.6 65.8 %evolve.1 = (f32[96,8,8,128]{3,2,1,0:T(8,128)}, f32[8,8,128]{2,1,0:T(8,128)}, f32[8,8,128]{2,1,0:T(8,128)}) custom-call(f32[96,8,8,128]{3,2,1,0:T(8,128)} %f_hbm.1, f32[96,8,8,128]{3,2,1,0:T(8,128)} %c_hbm.1), custom_call_target="tpu_custom_call" | custom-call | tf_op jit(solution)/shard_map/evolve/pallas_call | solution.py:245
  66.4 4.6 %finish.1 = (f32[96,8,8,128]{3,2,1,0:T(8,128)}, f32[96,8,8,128]{3,2,1,0:T(8,128)}) custom-call(f32[96,8,8,128]{3,2,1,0:T(8,128)} %get-tuple-element.5.end_ref, f32[8,8,128]{2,1,0:T(8,128)} %get-tuple-element.6.mean_ref, f32[8,8,128]{2,1,0:T(8,128)} %get-tuple-element.7.scale_ref), custom_call_target="tpu_custom_call" | custom-call | tf_op jit(solution)/shard_map/finish/pallas_call | solution.py:270
where the time goes:
time: 71.1 us
  Pallas kernels  70.4 us (99%)
    pallas_call x1, Pallas kernels, local(): pl.pallas_call(functools.partial(evolve, sizes), out_shape=(whole, line,...  65.8 us
    pallas_call x1, Pallas kernels, local(): pl.pallas_call(finish, out_shape=(whole, whole), in_specs=[vmem, vmem, vm...  4.62 us

commit v1 on v0

--- a/solution.py
+++ b/solution.py
@@ -95,6 +95,7 @@
         def row(step, _):
             y = chunk * part + step
             centre = [field[slot, y + 1, x, inner_z] for x in range(width + 2)]
+            values = []
             for x in range(width):
                 value = centre[x + 1]
                 around = (
@@ -102,7 +103,9 @@
                     + (centre[x] + centre[x + 2])
                     + (field[slot, y + 1, x + 1, pl.ds(Z - 1, depth)] + field[slot, y + 1, x + 1, pl.ds(Z + 1, depth)])
                 )
-                store(y, x, 0.1 * around + value * (0.6 - (0.2 * value) * crowd[y, x]))
+                values.append(0.1 * around + value * (0.6 - (0.2 * value) * crowd[y, x]))
+            for x in range(width):
+                store(y, x, values[x])
             return 0
 
         lax.fori_loop(0, part, row, 0)
@@ -244,7 +247,7 @@
     plane = pltpu.VMEM((width, depth, lanes), jnp.float32)
     end, mean, scale = pl.pallas_call(
         functools.partial(evolve, sizes),
-        out_shape=(whole, line, line),
+        out_shape=tuple(pltpu.VMEM(kind.shape, jnp.float32) for kind in (whole, line, line)),
         in_specs=[anywhere, anywhere],
         out_specs=(vmem, vmem, vmem),
         scratch_shapes=[
@@ -278,7 +281,7 @@
             pltpu.SemaphoreType.DMA,
         ],
         name="finish",
-    )(end, mean, scale)
+    )(*(pltpu.with_memory_space_constraint(value, pltpu.VMEM) for value in (end, mean, scale)))
 
 
 def solution(mesh):

time: 71.1 us -> 67.6 us (0.951)
  Pallas kernels: 70.4 us -> 66.9 us
    pallas_call x1, Pallas kernels: 4.62 us -> 2.71 us  [local(): pl.pallas_call(finish, out_shape=(whole, whole), in_specs=[vmem, vmem, vm...]
    pallas_call x1, Pallas kernels: 65.8 us -> 64.2 us  [local(): pl.pallas_call(functools.partial(evolve, sizes), out_shape=tuple((pltpu.V...]
where the time goes in v1:
time: 67.6 us; the launch traced here: 67.5 us
  Pallas kernels  66.9 us (99%)
    pallas_call x1, Pallas kernels, local(): pl.pallas_call(functools.partial(evolve, sizes), out_shape=tuple((pltpu.V...  64.2 us
    pallas_call x1, Pallas kernels, local(): pl.pallas_call(finish, out_shape=(whole, whole), in_specs=[vmem, vmem, vm...  2.71 us

profile of v1, /device:TPU:1, one launch (start us, length us, event | category | flops | bytes accessed | tf_op | source)
XLA Modules:
  0.0 67.5 jit_solution(4830200722045645635)
XLA Ops:
  0.6 64.2 %evolve.1 = (f32[96,8,8,128]{3,2,1,0:T(8,128)S(1)}, f32[8,8,128]{2,1,0:T(8,128)S(1)}, f32[8,8,128]{2,1,0:T(8,128)S(1)}) custom-call(f32[96,8,8,128]{3,2,1,0:T(8,128)} %f_hbm.1, f32[96,8,8,128]{3,2,1,0:T(8,128)} %c_hbm.1), custom_call_target="tpu_custom_call" | custom-call | tf_op jit(solution)/shard_map/evolve/pallas_call | solution.py:248
  64.8 2.7 %finish.1 = (f32[96,8,8,128]{3,2,1,0:T(8,128)}, f32[96,8,8,128]{3,2,1,0:T(8,128)}) custom-call(f32[96,8,8,128]{3,2,1,0:T(8,128)S(1)} %get-tuple-element.5.end_ref, f32[8,8,128]{2,1,0:T(8,128)S(1)} %get-tuple-element.6.mean_ref, f32[8,8,128]{2,1,0:T(8,128)S(1)} %get-tuple-element.7.scale_ref), custom_call_target="tpu_custom_call" | custom-call | tf_op jit(solution)/shard_map/finish/pallas_call | solution.py:273

commit v2 on v1

--- a/solution.py
+++ b/solution.py
@@ -13,8 +13,8 @@
 Z = 8
 
 
-def evolve(sizes, f_hbm, c_hbm, end_ref, mean_ref, scale_ref, field, crowd, shift, first, second,
-           mine, theirs, load_sem, crowd_sem, send_sem, recv_sem, row_send, row_recv, stat_send, stat_recv):
+def evolve(sizes, f_hbm, c_hbm, end_ref, mine, theirs, field, crowd, shift, first, second, load_sem, crowd_sem,
+           send_sem, recv_sem, row_send, row_recv, stat_send, stat_recv):
     rows, cols, slabs = sizes
     height, width, depth, _ = f_hbm.shape
     part = height // CHUNKS
@@ -110,14 +110,11 @@
 
         lax.fori_loop(0, part, row, 0)
 
-    for chunk in range(CHUNKS):
-        load(chunk).start()
-    for chunk in range(CHUNKS):
-        load_crowd(chunk).start()
-
     barrier = pltpu.get_barrier_semaphore()
     for peer in peers + (partner,):
         pl.semaphore_signal(barrier, inc=1, device_id=peer, device_id_type=MESH)
+    for chunk in range(CHUNKS):
+        load(chunk).start()
     pl.semaphore_wait(barrier, len(peers) + 1)
 
     def begin(chunk, _):
@@ -126,6 +123,8 @@
         return 0
 
     lax.fori_loop(0, CHUNKS, begin, 0)
+    for chunk in range(CHUNKS):
+        load_crowd(chunk).start()
 
     def loaded(chunk, _):
         load_crowd(chunk).wait()
@@ -207,23 +206,27 @@
 
     lax.fori_loop(0, CHUNKS, drain, 0)
     swap.wait()
+
+
+def finish(end_ref, mine, theirs, standardized_hbm, end_hbm, standardized, mean_ref, scale_ref, out_sem, end_sem):
+    height, width = end_ref.shape[:2]
+    part = height // CHUNKS
+
+    def copy_end(chunk):
+        part_rows = pl.ds(chunk * part, part)
+        return pltpu.make_async_copy(end_ref.at[part_rows], end_hbm.at[part_rows], end_sem.at[chunk])
+
+    def copy_out(chunk):
+        part_rows = pl.ds(chunk * part, part)
+        return pltpu.make_async_copy(standardized.at[part_rows], standardized_hbm.at[part_rows], out_sem.at[chunk])
+
+    for chunk in range(CHUNKS):
+        copy_end(chunk).start()
     for x in range(width):
         apart = mine[0, x] - theirs[0, x]
         total = mine[1, x] + theirs[1, x] + apart * apart * (0.5 * height)
         mean_ref[x] = 0.5 * (mine[0, x] + theirs[0, x])
         scale_ref[x] = lax.rsqrt(total * (0.5 / height) + 0.0001)
-
-
-def finish(end_ref, mean_ref, scale_ref, standardized_hbm, end_hbm, standardized, out_sem, end_sem):
-    height, width = end_ref.shape[:2]
-    part = height // CHUNKS
-    copy_end = pltpu.make_async_copy(end_ref, end_hbm, end_sem)
-
-    def copy_out(chunk):
-        part_rows = pl.ds(chunk * part, part)
-        return pltpu.make_async_copy(standardized.at[part_rows], standardized_hbm.at[part_rows], out_sem.at[chunk])
-
-    copy_end.start()
     for chunk in range(CHUNKS):
 
         def row(step, _):
@@ -236,18 +239,19 @@
         copy_out(chunk).start()
     for chunk in range(CHUNKS):
         copy_out(chunk).wait()
-    copy_end.wait()
+    for chunk in range(CHUNKS):
+        copy_end(chunk).wait()
 
 
 def local(sizes, field_values, crowding):
     height, width, depth, lanes = field_values.shape
     whole = jax.ShapeDtypeStruct(field_values.shape, jnp.float32)
-    line = jax.ShapeDtypeStruct((width, depth, lanes), jnp.float32)
+    pair = jax.ShapeDtypeStruct((2, width, depth, lanes), jnp.float32)
     vmem, anywhere = pl.BlockSpec(memory_space=pltpu.VMEM), pl.BlockSpec(memory_space=pl.ANY)
     plane = pltpu.VMEM((width, depth, lanes), jnp.float32)
-    end, mean, scale = pl.pallas_call(
+    end, mine, theirs = pl.pallas_call(
         functools.partial(evolve, sizes),
-        out_shape=tuple(pltpu.VMEM(kind.shape, jnp.float32) for kind in (whole, line, line)),
+        out_shape=tuple(pltpu.VMEM(kind.shape, jnp.float32) for kind in (whole, pair, pair)),
         in_specs=[anywhere, anywhere],
         out_specs=(vmem, vmem, vmem),
         scratch_shapes=[
@@ -256,8 +260,6 @@
             plane,
             plane,
             plane,
-            pltpu.VMEM((2, width, depth, lanes), jnp.float32),
-            pltpu.VMEM((2, width, depth, lanes), jnp.float32),
             pltpu.SemaphoreType.DMA((CHUNKS,)),
             pltpu.SemaphoreType.DMA((CHUNKS,)),
             pltpu.SemaphoreType.DMA((2, CHUNKS, 4)),
@@ -277,11 +279,13 @@
         out_specs=(anywhere, anywhere),
         scratch_shapes=[
             pltpu.VMEM((height, width, depth, lanes), jnp.float32),
+            plane,
+            plane,
             pltpu.SemaphoreType.DMA((CHUNKS,)),
-            pltpu.SemaphoreType.DMA,
+            pltpu.SemaphoreType.DMA((CHUNKS,)),
         ],
         name="finish",
-    )(*(pltpu.with_memory_space_constraint(value, pltpu.VMEM) for value in (end, mean, scale)))
+    )(*(pltpu.with_memory_space_constraint(value, pltpu.VMEM) for value in (end, mine, theirs)))
 
 
 def solution(mesh):

time: 67.6 us -> 67.6 us (level)
  no operation moved by 1% of the time
where the time goes in v2:
time: 67.6 us; the launch traced here: 67.5 us
  Pallas kernels  66.9 us (99%)
    pallas_call x1, Pallas kernels, local(): pl.pallas_call(functools.partial(evolve, sizes), out_shape=tuple((pltpu.V...  64.1 us
    pallas_call x1, Pallas kernels, local(): pl.pallas_call(finish, out_shape=(whole, whole), in_specs=[vmem, vmem, vm...  2.76 us

profile of v2, /device:TPU:1, one launch (start us, length us, event | category | flops | bytes accessed | tf_op | source)
XLA Modules:
  0.0 67.5 jit_solution(10977883931879417334)
XLA Ops:
  0.6 64.1 %evolve.1 = (f32[96,8,8,128]{3,2,1,0:T(8,128)S(1)}, f32[2,8,8,128]{3,2,1,0:T(8,128)S(1)}, f32[2,8,8,128]{3,2,1,0:T(8,128)S(1)}) custom-call(f32[96,8,8,128]{3,2,1,0:T(8,128)} %f_hbm.1, f32[96,8,8,128]{3,2,1,0:T(8,128)} %c_hbm.1), custom_call_target="tpu_custom_call" | custom-call | tf_op jit(solution)/shard_map/evolve/pallas_call | solution.py:252
  64.8 2.8 %finish.1 = (f32[96,8,8,128]{3,2,1,0:T(8,128)}, f32[96,8,8,128]{3,2,1,0:T(8,128)}) custom-call(f32[96,8,8,128]{3,2,1,0:T(8,128)S(1)} %get-tuple-element.5.end_ref, f32[2,8,8,128]{3,2,1,0:T(8,128)S(1)} %get-tuple-element.6.mine, f32[2,8,8,128]{3,2,1,0:T(8,128)S(1)} %get-tuple-element.7.theirs), custom_call_target="tpu_custom_call" | custom-call | tf_op jit(solution)/shard_map/finish/pallas_call | solution.py:275

commit v3 on v2

--- a/solution.py
+++ b/solution.py
@@ -137,7 +137,7 @@
         other = 1 - slot
 
         def one_chunk(place, _):
-            chunk = lax.rem(place + step, CHUNKS)
+            chunk = place
             arrived(slot, chunk)
 
             @pl.when(step > 0)
@@ -160,7 +160,7 @@
     slot = step % 2
 
     def last_chunk(place, _):
-        chunk = lax.rem(place + step, CHUNKS)
+        chunk = place
         arrived(slot, chunk)
 
         def store(y, x, value):

time: 67.6 us -> 67.2 us (level)
  no operation moved by 1% of the time
where the time goes in v3:
time: 67.2 us; the launch traced here: 67.1 us
  Pallas kernels  66.5 us (99%)
    pallas_call x1, Pallas kernels, local(): pl.pallas_call(functools.partial(evolve, sizes), out_shape=tuple((pltpu.V...  63.7 us
    pallas_call x1, Pallas kernels, local(): pl.pallas_call(finish, out_shape=(whole, whole), in_specs=[vmem, vmem, vm...  2.76 us

profile of v3, /device:TPU:1, one launch (start us, length us, event | category | flops | bytes accessed | tf_op | source)
XLA Modules:
  0.0 67.1 jit_solution(7102804665799274503)
XLA Ops:
  0.6 63.7 %evolve.1 = (f32[96,8,8,128]{3,2,1,0:T(8,128)S(1)}, f32[2,8,8,128]{3,2,1,0:T(8,128)S(1)}, f32[2,8,8,128]{3,2,1,0:T(8,128)S(1)}) custom-call(f32[96,8,8,128]{3,2,1,0:T(8,128)} %f_hbm.1, f32[96,8,8,128]{3,2,1,0:T(8,128)} %c_hbm.1), custom_call_target="tpu_custom_call" | custom-call | tf_op jit(solution)/shard_map/evolve/pallas_call | solution.py:252
  64.3 2.8 %finish.1 = (f32[96,8,8,128]{3,2,1,0:T(8,128)}, f32[96,8,8,128]{3,2,1,0:T(8,128)}) custom-call(f32[96,8,8,128]{3,2,1,0:T(8,128)S(1)} %get-tuple-element.5.end_ref, f32[2,8,8,128]{3,2,1,0:T(8,128)S(1)} %get-tuple-element.6.mine, f32[2,8,8,128]{3,2,1,0:T(8,128)S(1)} %get-tuple-element.7.theirs), custom_call_target="tpu_custom_call" | custom-call | tf_op jit(solution)/shard_map/finish/pallas_call | solution.py:275

commit v4 on v3

--- a/solution.py
+++ b/solution.py
@@ -13,7 +13,7 @@
 Z = 8
 
 
-def evolve(sizes, f_hbm, c_hbm, end_ref, mine, theirs, field, crowd, shift, first, second, load_sem, crowd_sem,
+def evolve(sizes, f_hbm, c_hbm, end_ref, mine, theirs, field, crowd, shift, first, second,
            send_sem, recv_sem, row_send, row_recv, stat_send, stat_recv):
     rows, cols, slabs = sizes
     height, width, depth, _ = f_hbm.shape
@@ -32,12 +32,12 @@
         return pltpu.make_async_copy(
             f_hbm.at[pl.ds(chunk * part, part)],
             field.at[0, pl.ds(1 + chunk * part, part), inner_x, inner_z],
-            load_sem.at[chunk],
+            send_sem.at[1, chunk],
         )
 
     def load_crowd(chunk):
         part_rows = pl.ds(chunk * part, part)
-        return pltpu.make_async_copy(c_hbm.at[part_rows], crowd.at[part_rows], crowd_sem.at[chunk])
+        return pltpu.make_async_copy(c_hbm.at[part_rows], crowd.at[part_rows], send_sem.at[1, chunk])
 
     def face(slot, chunk, side):
         part_rows = pl.ds(1 + chunk * part, part)
@@ -50,8 +50,8 @@
         return pltpu.make_async_remote_copy(
             src_ref=field.at[(slot, part_rows) + source],
             dst_ref=field.at[(slot, part_rows) + target],
-            send_sem=send_sem.at[slot, chunk, side],
-            recv_sem=recv_sem.at[slot, chunk, side],
+            send_sem=send_sem.at[slot, chunk],
+            recv_sem=recv_sem.at[slot, chunk],
             device_id=peers[side],
             device_id_type=MESH,
         )
@@ -81,14 +81,16 @@
             face(slot, chunk, side).start()
         on_edges(chunk, lambda side: edge_row(slot, side).start())
 
+    def wait_faces(sem):
+        four_faces = crowd.at[pl.ds(0, part * 2 * (width + depth) // (width * depth))]
+        pltpu.make_async_copy(four_faces, four_faces, sem).wait()
+
     def sent(slot, chunk):
-        for side in range(4):
-            face(slot, chunk, side).wait_send()
+        wait_faces(send_sem.at[slot, chunk])
         on_edges(chunk, lambda side: edge_row(slot, side).wait_send())
 
     def arrived(slot, chunk):
-        for side in range(4):
-            face(slot, chunk, side).wait_recv()
+        wait_faces(recv_sem.at[slot, chunk])
         on_edges(chunk, lambda side: edge_row(slot, 1 - side).wait_recv())
 
     def advance(slot, chunk, store):
@@ -212,16 +214,13 @@
     height, width = end_ref.shape[:2]
     part = height // CHUNKS
 
-    def copy_end(chunk):
-        part_rows = pl.ds(chunk * part, part)
-        return pltpu.make_async_copy(end_ref.at[part_rows], end_hbm.at[part_rows], end_sem.at[chunk])
+    copy_end = pltpu.make_async_copy(end_ref, end_hbm, end_sem)
 
     def copy_out(chunk):
         part_rows = pl.ds(chunk * part, part)
-        return pltpu.make_async_copy(standardized.at[part_rows], standardized_hbm.at[part_rows], out_sem.at[chunk])
-
-    for chunk in range(CHUNKS):
-        copy_end(chunk).start()
+        return pltpu.make_async_copy(standardized.at[part_rows], standardized_hbm.at[part_rows], out_sem)
+
+    copy_end.start()
     for x in range(width):
         apart = mine[0, x] - theirs[0, x]
         total = mine[1, x] + theirs[1, x] + apart * apart * (0.5 * height)
@@ -237,10 +236,8 @@
 
         lax.fori_loop(0, part, row, 0)
         copy_out(chunk).start()
-    for chunk in range(CHUNKS):
-        copy_out(chunk).wait()
-    for chunk in range(CHUNKS):
-        copy_end(chunk).wait()
+    pltpu.make_async_copy(standardized, standardized_hbm, out_sem).wait()
+    copy_end.wait()
 
 
 def local(sizes, field_values, crowding):
@@ -260,10 +257,8 @@
             plane,
             plane,
             plane,
-            pltpu.SemaphoreType.DMA((CHUNKS,)),
-            pltpu.SemaphoreType.DMA((CHUNKS,)),
-            pltpu.SemaphoreType.DMA((2, CHUNKS, 4)),
-            pltpu.SemaphoreType.DMA((2, CHUNKS, 4)),
+            pltpu.SemaphoreType.DMA((2, CHUNKS)),
+            pltpu.SemaphoreType.DMA((2, CHUNKS)),
             pltpu.SemaphoreType.DMA((2, 2)),
             pltpu.SemaphoreType.DMA((2, 2)),
             pltpu.SemaphoreType.DMA,
@@ -281,8 +276,8 @@
             pltpu.VMEM((height, width, depth, lanes), jnp.float32),
             plane,
             plane,
-            pltpu.SemaphoreType.DMA((CHUNKS,)),
-            pltpu.SemaphoreType.DMA((CHUNKS,)),
+            pltpu.SemaphoreType.DMA,
+            pltpu.SemaphoreType.DMA,
         ],
         name="finish",
     )(*(pltpu.with_memory_space_constraint(value, pltpu.VMEM) for value in (end, mine, theirs)))

time: 67.2 us -> 66.4 us (0.988)
  Pallas kernels: 66.5 us -> 65.6 us
    pallas_call x1, Pallas kernels: 63.7 us -> 63 us  [local(): pl.pallas_call(functools.partial(evolve, sizes), out_shape=tuple((pltpu.V...]
where the time goes in v4:
time: 66.4 us; the launch traced here: 66.3 us
  Pallas kernels  65.6 us (99%)
    pallas_call x1, Pallas kernels, local(): pl.pallas_call(functools.partial(evolve, sizes), out_shape=tuple((pltpu.V...  63 us
    pallas_call x1, Pallas kernels, local(): pl.pallas_call(finish, out_shape=(whole, whole), in_specs=[vmem, vmem, vm...  2.67 us

profile of v4, /device:TPU:1, one launch (start us, length us, event | category | flops | bytes accessed | tf_op | source)
XLA Modules:
  0.0 66.3 jit_solution(18272280944185461320)
XLA Ops:
  0.6 63.0 %evolve.1 = (f32[96,8,8,128]{3,2,1,0:T(8,128)S(1)}, f32[2,8,8,128]{3,2,1,0:T(8,128)S(1)}, f32[2,8,8,128]{3,2,1,0:T(8,128)S(1)}) custom-call(f32[96,8,8,128]{3,2,1,0:T(8,128)} %f_hbm.1, f32[96,8,8,128]{3,2,1,0:T(8,128)} %c_hbm.1), custom_call_target="tpu_custom_call" | custom-call | tf_op jit(solution)/shard_map/evolve/pallas_call | solution.py:249
  63.6 2.7 %finish.1 = (f32[96,8,8,128]{3,2,1,0:T(8,128)}, f32[96,8,8,128]{3,2,1,0:T(8,128)}) custom-call(f32[96,8,8,128]{3,2,1,0:T(8,128)S(1)} %get-tuple-element.5.end_ref, f32[2,8,8,128]{3,2,1,0:T(8,128)S(1)} %get-tuple-element.6.mine, f32[2,8,8,128]{3,2,1,0:T(8,128)S(1)} %get-tuple-element.7.theirs), custom_call_target="tpu_custom_call" | custom-call | tf_op jit(solution)/shard_map/finish/pallas_call | solution.py:270

commit v5 on v4

--- a/solution.py
+++ b/solution.py
@@ -8,7 +8,7 @@
 from jax.sharding import PartitionSpec as P
 
 STEPS = 6
-CHUNKS = 6
+CHUNKS = 12
 MESH = pl.DeviceIdType.MESH
 Z = 8
 
@@ -32,12 +32,10 @@
         return pltpu.make_async_copy(
             f_hbm.at[pl.ds(chunk * part, part)],
             field.at[0, pl.ds(1 + chunk * part, part), inner_x, inner_z],
-            send_sem.at[1, chunk],
+            send_sem.at[chunk],
         )
 
-    def load_crowd(chunk):
-        part_rows = pl.ds(chunk * part, part)
-        return pltpu.make_async_copy(c_hbm.at[part_rows], crowd.at[part_rows], send_sem.at[1, chunk])
+    load_crowd = pltpu.make_async_copy(c_hbm, crowd, stat_send)
 
     def face(slot, chunk, side):
         part_rows = pl.ds(1 + chunk * part, part)
@@ -50,7 +48,7 @@
         return pltpu.make_async_remote_copy(
             src_ref=field.at[(slot, part_rows) + source],
             dst_ref=field.at[(slot, part_rows) + target],
-            send_sem=send_sem.at[slot, chunk],
+            send_sem=send_sem.at[chunk],
             recv_sem=recv_sem.at[slot, chunk],
             device_id=peers[side],
             device_id_type=MESH,
@@ -61,7 +59,7 @@
         return pltpu.make_async_remote_copy(
             src_ref=field.at[slot, source, inner_x, inner_z],
             dst_ref=field.at[slot, target, inner_x, inner_z],
-            send_sem=row_send.at[slot, side],
+            send_sem=row_send.at[side],
             recv_sem=row_recv.at[slot, side],
             device_id=partner,
             device_id_type=MESH,
@@ -85,9 +83,9 @@
         four_faces = crowd.at[pl.ds(0, part * 2 * (width + depth) // (width * depth))]
         pltpu.make_async_copy(four_faces, four_faces, sem).wait()
 
-    def sent(slot, chunk):
-        wait_faces(send_sem.at[slot, chunk])
-        on_edges(chunk, lambda side: edge_row(slot, side).wait_send())
+    def sent(chunk):
+        wait_faces(send_sem.at[chunk])
+        on_edges(chunk, lambda side: edge_row(0, side).wait_send())
 
     def arrived(slot, chunk):
         wait_faces(recv_sem.at[slot, chunk])
@@ -125,14 +123,8 @@
         return 0
 
     lax.fori_loop(0, CHUNKS, begin, 0)
-    for chunk in range(CHUNKS):
-        load_crowd(chunk).start()
-
-    def loaded(chunk, _):
-        load_crowd(chunk).wait()
-        return 0
-
-    lax.fori_loop(0, CHUNKS, loaded, 0)
+    load_crowd.start()
+    load_crowd.wait()
 
     def one_step(step, _):
         slot = lax.rem(step, 2)
@@ -142,14 +134,11 @@
             chunk = place
             arrived(slot, chunk)
 
-            @pl.when(step > 0)
-            def _():
-                sent(other, chunk)
-
             def store(y, x, value):
                 field[other, y + 1, x + 1, inner_z] = value
 
             advance(slot, chunk, store)
+            sent(chunk)
             send(other, chunk)
             return 0
 
@@ -202,8 +191,7 @@
     swap.start()
 
     def drain(chunk, _):
-        sent(1 - slot, chunk)
-        sent(slot, chunk)
+        sent(chunk)
         return 0
 
     lax.fori_loop(0, CHUNKS, drain, 0)
@@ -257,9 +245,9 @@
             plane,
             plane,
             plane,
+            pltpu.SemaphoreType.DMA((CHUNKS,)),
             pltpu.SemaphoreType.DMA((2, CHUNKS)),
-            pltpu.SemaphoreType.DMA((2, CHUNKS)),
-            pltpu.SemaphoreType.DMA((2, 2)),
+            pltpu.SemaphoreType.DMA((2,)),
             pltpu.SemaphoreType.DMA((2, 2)),
             pltpu.SemaphoreType.DMA,
             pltpu.SemaphoreType.DMA,

time: 66.4 us -> 66.3 us (level)
  no operation moved by 1% of the time
where the time goes in v5:
time: 66.3 us; the launch traced here: 66.1 us
  Pallas kernels  65.5 us (99%)
    pallas_call x1, Pallas kernels, local(): pl.pallas_call(functools.partial(evolve, sizes), out_shape=tuple((pltpu.V...  62.9 us
    pallas_call x1, Pallas kernels, local(): pl.pallas_call(finish, out_shape=(whole, whole), in_specs=[vmem, vmem, vm...  2.65 us

profile of v5, /device:TPU:1, one launch (start us, length us, event | category | flops | bytes accessed | tf_op | source)
XLA Modules:
  0.0 66.1 jit_solution(17501526504714667353)
XLA Ops:
  0.6 62.9 %evolve.1 = (f32[96,8,8,128]{3,2,1,0:T(8,128)S(1)}, f32[2,8,8,128]{3,2,1,0:T(8,128)S(1)}, f32[2,8,8,128]{3,2,1,0:T(8,128)S(1)}) custom-call(f32[96,8,8,128]{3,2,1,0:T(8,128)} %f_hbm.1, f32[96,8,8,128]{3,2,1,0:T(8,128)} %c_hbm.1), custom_call_target="tpu_custom_call" | custom-call | tf_op jit(solution)/shard_map/evolve/pallas_call | solution.py:237
  63.5 2.7 %finish.1 = (f32[96,8,8,128]{3,2,1,0:T(8,128)}, f32[96,8,8,128]{3,2,1,0:T(8,128)}) custom-call(f32[96,8,8,128]{3,2,1,0:T(8,128)S(1)} %get-tuple-element.5.end_ref, f32[2,8,8,128]{3,2,1,0:T(8,128)S(1)} %get-tuple-element.6.mine, f32[2,8,8,128]{3,2,1,0:T(8,128)S(1)} %get-tuple-element.7.theirs), custom_call_target="tpu_custom_call" | custom-call | tf_op jit(solution)/shard_map/finish/pallas_call | solution.py:258
